TPU v7x, 32 devices: a whole 2x2x4 slice. The times are simulated.
32 devices in a mesh: row: 2 (over x), col: 4 (over z), layer: 4 (over y, core).
Axes of the slice: x: 2, y: 2, z: 4, core: 2. Of those that a mesh axis runs over, the one named last changes fastest.
Arguments:
- left_factor: float32 [2048, 4096], P('row', ('layer', 'col')), may hold values from 0.01 to 1
- right_factor: float32 [4096, 4096], P(('layer', 'row'), 'col'), may hold values from 0.01 to 1
- left_occupancy: int32 [16, 32], replicated, may hold values 0 or 1
- right_occupancy: int32 [32, 32], replicated, may hold values 0 or 1
Outputs:
- flow: float32 [2048, 4096], P(('row', 'layer'), 'col')
All inputs are finite; a program needn't handle non-finite values.
Results may differ from a plain program's by a relative error of at most 0.000082.
Values sent between devices are 32-bit elements; how exact they have to be, the bound alone decides.
No kernel may reach another device: no remote copies, remote signals or barrier semaphores. Data moves between devices by JAX's collectives and lax.ppermute only.
A program may use at most 64 MiB of HBM per device.

v0:
```python
import jax
import jax.numpy as jnp
from jax import lax
from jax.sharding import PartitionSpec as P

BLOCK = 128
EPSILON = 1e-06


def widen(flags):
    return jnp.repeat(jnp.repeat(flags.astype(jnp.float32), BLOCK, 0), BLOCK, 1)


def on_device(left_factor, right_factor, left_occupancy, right_occupancy):
    row_index = lax.axis_index("row")
    col_index = lax.axis_index("col")
    layer_index = lax.axis_index("layer")
    right_whole = lax.all_gather(right_factor, "row", axis=0, tiled=True)
    depth = right_whole.shape[0]
    width = right_whole.shape[1]
    depth_blocks = depth // BLOCK
    width_blocks = width // BLOCK
    right_flags = lax.dynamic_slice(
        right_occupancy,
        (layer_index * depth_blocks, col_index * width_blocks),
        (depth_blocks, width_blocks),
    )
    right_masked = right_whole * widen(right_flags)
    band_rows = left_factor.shape[0]
    row_blocks = band_rows // BLOCK
    left_flags = lax.dynamic_slice(
        left_occupancy,
        (row_index * row_blocks, layer_index * depth_blocks),
        (row_blocks, depth_blocks),
    )
    left_mask = widen(left_flags)
    left_whole = lax.all_gather(left_factor, "col", axis=1, tiled=True)
    left_masked = left_whole * left_mask
    owned = lax.psum_scatter(
        jnp.dot(
            left_masked,
            right_masked,
            precision=lax.Precision.HIGHEST,
            preferred_element_type=jnp.float32,
        ),
        "layer",
        scatter_dimension=0,
        tiled=True,
    )
    squared = owned * owned
    totals = lax.psum(jnp.sum(squared, axis=0), ("row", "layer"))
    total_rows = band_rows * lax.axis_size("row")
    return total_rows * squared / (totals + EPSILON)


def solution(mesh):
    return jax.shard_map(
        on_device,
        mesh=mesh,
        in_specs=(P("row", ("layer", "col")), P(("layer", "row"), "col"), P(), P()),
        out_specs=P(("row", "layer"), "col"),
        check_vma=False,
    )
```

profile of v0, /device:TPU:0, one launch (start us, length us, event | category | flops | bytes accessed | tf_op | source)
XLA Modules:
  0.0 237.0 jit_solution(607008218345202250)
XLA Ops:
  6.5 0.0 all-gather.5.cloned.1.call-start
  6.5 0.7 all-gather.5.cloned.1.call-update
  7.3 0.0 all-gather.3.cloned.1.call-start
  7.3 0.7 all-gather.3.cloned.1.call-update
  8.0 0.0 reduce-scatter.2.cloned.1.call-start
  8.1 0.8 dynamic-slice_convert_fusion
  8.8 59.5 %all-gather.5.cloned.1.call-done = f32[1024,1024]{1,0:T(8,128)} async-done(((f32[512,1024]{1,0:T(8,128)}), f32[1024,1024]{1,0:T(8,128)}) %all-gather.5.cloned.1.call-update) | async-done | bytes 4194320 | tf_op jit(solution)/shard_map/all_gather | solution.py:18
  68.4 82.3 %all-gather.3.cloned.1.call-done = f32[1024,1024]{1,0:T(8,128)} async-done(((f32[1024,256]{1,0:T(8,128)}), f32[1024,1024]{1,0:T(8,128)}) %all-gather.3.cloned.1.call-update) | async-done | bytes 4194320 | tf_op jit(solution)/shard_map/all_gather | solution.py:37
  150.7 0.0 copy-start
  150.7 0.0 copy-start.1
  150.8 1.1 broadcast_in_dim.14
  151.9 1.1 broadcast_in_dim.16
  153.1 0.0 copy-done
  153.1 1.1 copy-done.1
  154.2 16.8 %fusion = f32[1024,1024]{1,0:T(8,128)} fusion(f32[1024,1024]{1,0:T(8,128)S(1)} %copy-done, f32[128,8,8,128]{3,2,1,0:T(8,128)S(1)} %bitcast.11, f32[1024,1024]{1,0:T(8,128)S(1)} %copy-done.1, f32[128,8,8,128]{3,2,1,0:T(8,128)S(1)} %bitcast.10), kind=kOutput, calls=%fused_computation.1 | convolution fusion | flops 12886999040 | bytes 20971520 | tf_op jit(solution)/shard_map/dot_general | solution.py:40
  171.0 0.0 reduce-scatter.2.cloned.1.call-update
  171.0 43.2 %reduce-scatter.2.cloned.1.call-done = f32[256,1024]{1,0:T(8,128)} async-done(((f32[1024,1024]{1,0:T(8,128)}), f32[256,1024]{1,0:T(8,128)}) %reduce-scatter.2.cloned.1.call-update) | async-done | bytes 1048592 | tf_op jit(solution)/shard_map/reduce_scatter | solution.py:39
  214.3 1.3 multiply_reduce_fusion
  215.6 12.5 %psum.7 = f32[1024]{0:T(1024)S(1)} all-reduce(f32[1024]{0:T(1024)S(1)} %multiply_reduce_fusion), channel_id=1, replica_groups=mesh['row'=2,'col'=4,'layer'=4] {'row','layer'}, use_global_device_ids=true, to_apply=%region_2.0 | all-reduce | flops 1024 | bytes 8192 | tf_op jit(solution)/shard_map/psum | solution.py:51
  228.1 2.4 multiply_divide_fusion
  (3 shorter events, 0.1 us)
Async XLA Ops:
  6.5 61.8 %all-gather.5.cloned.1.call-start = ((), (), s32[]{:S(2)}) async-start(), calls=%async_computation.2 | async-start | bytes 6291456 | tf_op jit(solution)/shard_map/all_gather | solution.py:18
  7.3 143.4 %all-gather.3.cloned.1.call-start = ((), (), s32[]{:S(2)}) async-start(), calls=%async_computation.1 | async-start | bytes 5242880 | tf_op jit(solution)/shard_map/all_gather | solution.py:37
  8.0 206.3 %reduce-scatter.2.cloned.1.call-start = ((), (), s32[]{:S(2)}) async-start(), calls=%async_computation.3 | async-start | bytes 5242880 | tf_op jit(solution)/shard_map/reduce_scatter | solution.py:39
  150.7 2.3 copy-start
  150.7 3.5 %copy-start.1 = (f32[1024,1024]{1,0:T(8,128)S(1)}, f32[1024,1024]{1,0:T(8,128)}, u32[]{:S(2)}) copy-start(f32[1024,1024]{1,0:T(8,128)} %all-gather.3.cloned.1.call-done) | copy-start | bytes 12582916
Sparse Core Ops, SparseCore 0:
  8.9 59.4 all-gather.4
  69.9 80.7 all-gather.2
  171.2 43.0 reduce-scatter.1
where the time goes:
time: 237 us
  waiting for transfers between devices  186 us (78%)
  matrix products  16.8 us (7%)
  between operations  13.2 us (6%)
  blocking collectives  12.5 us (5%)
  other arithmetic  4.48 us (2%)
  local copies, waits for them, and re-layouts  3.47 us (1%)
    all_gather x1, waiting for transfers between devices, on_device(): left_whole = lax.all_gather(left_factor, 'col', axis=1, tiled=True)  82.3 us
    all_gather x1, waiting for transfers between devices, on_device(): right_whole = lax.all_gather(right_factor, 'row', axis=0, tiled=True)  59.5 us
    reduce_scatter x1, waiting for transfers between devices, on_device(): lax.psum_scatter(jnp.dot(left_masked, right_masked, precision=lax.Precisi...  43.2 us
    dot_general x1, matrix products, on_device(): jnp.dot(left_masked, right_masked, precision=lax.Precision.HIGHEST, prefe...  16.8 us
    psum x1, blocking collectives, on_device(): totals = lax.psum(jnp.sum(squared, axis=0), ('row', 'layer'))  12.5 us
  transfers between devices with their start and end apart: 3, of which 3 were waited for; matrix products, arithmetic and copies ran while one was open for 0% of the time, Pallas kernels for 0%

commit v1 on v0

--- a/solution.py
+++ b/solution.py
@@ -34,7 +34,12 @@
         (row_blocks, depth_blocks),
     )
     left_mask = widen(left_flags)
-    left_whole = lax.all_gather(left_factor, "col", axis=1, tiled=True)
+    ring = [left_factor]
+    for hop in range(3):
+        ring.append(lax.ppermute(ring[-1], "col", [(dev, (dev + 1) % 4) for dev in range(4)]))
+    left_whole = jnp.roll(
+        jnp.concatenate(ring[::-1], axis=1), (lax.axis_index("col") + 1) * ring[0].shape[1], axis=1
+    )
     left_masked = left_whole * left_mask
     owned = lax.psum_scatter(
         jnp.dot(

time: 237 us -> 184 us (0.78)
  waiting for transfers between devices: 186 us -> 119 us
  local copies, waits for them, and re-layouts: 3.47 us -> 13.8 us
  starting transfers between devices: 0.08 us -> 3.1 us
    all_gather x1 -> x0, waiting for transfers between devices: 82.3 us -> none  [on_device(): left_whole = lax.all_gather(left_factor, 'col', axis=1, tiled=True)]
    ppermute x0 -> x3, waiting for transfers between devices: none -> 76.1 us  [on_device(): lax.ppermute(ring[-1], 'col', [(dev, (dev + 1) % 4) for dev in range(4)])]
    all_gather x1, waiting for transfers between devices: 59.5 us -> 0.01 us  [on_device(): right_whole = lax.all_gather(right_factor, 'row', axis=0, tiled=True)]
    unnamed x4 -> x11, local copies, waits for them, and re-layouts: 1.12 us -> 10.4 us
    ppermute x0 -> x3, starting transfers between devices: none -> 3.06 us  [on_device(): lax.ppermute(ring[-1], 'col', [(dev, (dev + 1) % 4) for dev in range(4)])]
  transfers between devices with their start and end apart: 3 -> 5, of which waited for: 3 -> 4; matrix products, arithmetic and copies ran while one was open for 0% -> 7% of each run, Pallas kernels for 0% -> 0%
where the time goes in v1:
time: 184 us
  waiting for transfers between devices  119 us (65%)
  matrix products  17.9 us (10%)
  local copies, waits for them, and re-layouts  13.8 us (8%)
  between operations  13.4 us (7%)
  blocking collectives  12.5 us (7%)
  other arithmetic  4.47 us (2%)
  starting transfers between devices  3.1 us (2%)
    ppermute x3, waiting for transfers between devices, on_device(): lax.ppermute(ring[-1], 'col', [(dev, (dev + 1) % 4) for dev in range(4)])  76.1 us
    reduce_scatter x1, waiting for transfers between devices, on_device(): lax.psum_scatter(jnp.dot(left_masked, right_masked, precision=lax.Precisi...  42.7 us
    dot_general x1, matrix products, on_device(): jnp.dot(left_masked, right_masked, precision=lax.Precision.HIGHEST, prefe...  17.9 us
    psum x1, blocking collectives, on_device(): totals = lax.psum(jnp.sum(squared, axis=0), ('row', 'layer'))  12.5 us
    unnamed x11, local copies, waits for them, and re-layouts  10.4 us
  transfers between devices with their start and end apart: 5, of which 4 were waited for; matrix products, arithmetic and copies ran while one was open for 7% of the time, Pallas kernels for 0%

profile of v1, /device:TPU:0, one launch (start us, length us, event | category | flops | bytes accessed | tf_op | source)
XLA Modules:
  0.0 184.1 jit_solution(4659363931010956685)
XLA Ops:
  6.5 3.1 %collective-permute-start = (f32[1024,256]{1,0:T(8,128)}, f32[1024,256]{1,0:T(8,128)S(1)}, u32[]{:S(2)}, u32[]{:S(2)}) collective-permute-start(f32[1024,256]{1,0:T(8,128)} %param.4), channel_id=1, source_target_pairs={{0,4},{4,8},{8,12},{12,0},{1,5},{5,9},{9,13},{13,1},{2,6},{6,10},{... | collective-permute-start | bytes 3145736 | tf_op jit(solution)/shard_map/ppermute | solution.py:39
  9.6 0.0 all-gather.2.cloned.1.call-update
  9.6 0.0 reduce-scatter.2.cloned.1.call-start
  9.7 25.4 %collective-permute-done = f32[1024,256]{1,0:T(8,128)S(1)} collective-permute-done((f32[1024,256]{1,0:T(8,128)}, f32[1024,256]{1,0:T(8,128)S(1)}, u32[]{:S(2)}, u32[]{:S(2)}) %collective-permute-start) | collective-permute-done | bytes 1048608 | tf_op jit(solution)/shard_map/ppermute | solution.py:39
  35.1 0.0 collective-permute-start.1
  35.1 26.1 %collective-permute-done.1 = f32[1024,256]{1,0:T(8,128)S(1)} collective-permute-done((f32[1024,256]{1,0:T(8,128)S(1)}, f32[1024,256]{1,0:T(8,128)S(1)}, u32[]{:S(2)}, u32[]{:S(2)}) %collective-permute-start.1) | collective-permute-done | bytes 1048608 | tf_op jit(solution)/shard_map/ppermute | solution.py:39
  61.2 0.8 dynamic-slice_convert_fusion
  62.0 24.6 %collective-permute-done.2 = f32[1024,256]{1,0:T(8,128)} collective-permute-done((f32[1024,256]{1,0:T(8,128)S(1)}, f32[1024,256]{1,0:T(8,128)}, u32[]{:S(2)}, u32[]{:S(2)}) %collective-permute-start.2) | collective-permute-done | bytes 1048608 | tf_op jit(solution)/shard_map/ppermute | solution.py:39
  86.5 2.4 %constant_dynamic-update-slice_fusion.7 = f32[1024,2048]{1,0:T(8,128)} fusion(f32[1024,256]{1,0:T(8,128)} %collective-permute-done.2), kind=kLoop, calls=%fused_computation.15 | loop fusion | bytes 2097152
  88.9 1.1 constant_dynamic-update-slice_fusion.6
  90.1 1.1 constant_dynamic-update-slice_fusion.5
  91.2 1.2 constant_dynamic-update-slice_fusion.4
  92.3 2.4 %constant_dynamic-update-slice_fusion.3 = f32[1024,2048]{1,0:T(8,128)} fusion(f32[1024,2048]{1,0:T(8,128)} %constant_dynamic-update-slice_fusion.4, f32[1024,256]{1,0:T(8,128)} %collective-permute-done.2), kind=kLoop, calls=%fused_computation.11 | loop fusion | bytes 2097152
  94.7 1.1 constant_dynamic-update-slice_fusion.2
  95.8 1.1 constant_dynamic-update-slice_fusion.1
  96.9 1.1 constant_dynamic-update-slice_fusion
  98.1 1.1 broadcast_in_dim.14
  99.3 1.1 broadcast_in_dim.16
  100.4 17.9 %fusion = f32[1024,1024]{1,0:T(8,128)} fusion(f32[1024,1024]{1,0:T(8,128)S(1)} %copy-done.1, f32[128,8,8,128]{3,2,1,0:T(8,128)S(1)} %bitcast.11, f32[128,8,8,128]{3,2,1,0:T(8,128)S(1)} %bitcast.10, f32[1024,2048]{1,0:T(8,128)} %constant_dynamic-update-slice_fusion, s32[]{:T(128)S(6)} %select_n.24), kind=kOutput, calls=%fused_computation.1 | convolution fusion | flops 12886999040 | bytes 20971524 | tf_op jit(solution)/shard_map/dot_general | solution.py:45
  118.3 0.0 reduce-scatter.2.cloned.1.call-update
  118.4 42.7 %reduce-scatter.2.cloned.1.call-done = f32[256,1024]{1,0:T(8,128)} async-done(((f32[1024,1024]{1,0:T(8,128)}), f32[256,1024]{1,0:T(8,128)}) %reduce-scatter.2.cloned.1.call-update) | async-done | bytes 1048592 | tf_op jit(solution)/shard_map/reduce_scatter | solution.py:44
  161.0 1.3 multiply_reduce_fusion
  162.3 12.5 %psum.7 = f32[1024]{0:T(1024)S(1)} all-reduce(f32[1024]{0:T(1024)S(1)} %multiply_reduce_fusion), channel_id=1, replica_groups=mesh['row'=2,'col'=4,'layer'=4] {'row','layer'}, use_global_device_ids=true, to_apply=%region_2.3 | all-reduce | flops 1024 | bytes 8192 | tf_op jit(solution)/shard_map/psum | solution.py:56
  174.9 2.4 %multiply_divide_fusion = f32[256,1024]{1,0:T(8,128)} fusion(f32[256,1024]{1,0:T(8,128)} %reduce-scatter.2.cloned.1.call-done, f32[1024]{0:T(1024)S(1)} %broadcast_add_fusion), kind=kLoop, calls=%fused_computation.6 | loop fusion | flops 786432 | bytes 2101248 | tf_op jit(solution)/shard_map/div | solution.py:58
  (10 shorter events, 0.1 us)
Async XLA Ops:
  6.5 84.7 %copy-start = (f32[1024,256]{1,0:T(8,128)S(1)}, f32[1024,256]{1,0:T(8,128)}, u32[]{:S(2)}) copy-start(f32[1024,256]{1,0:T(8,128)} %param.4) | copy-start | bytes 3145732
  6.5 91.5 %all-gather.2.cloned.1.call-start = ((), (), s32[]{:S(2)}) async-start(), calls=%async_computation.1 | async-start | bytes 6291456 | tf_op jit(solution)/shard_map/all_gather | solution.py:18
  6.5 28.5 %collective-permute-start = (f32[1024,256]{1,0:T(8,128)}, f32[1024,256]{1,0:T(8,128)S(1)}, u32[]{:S(2)}, u32[]{:S(2)}) collective-permute-start(f32[1024,256]{1,0:T(8,128)} %param.4), channel_id=1, source_target_pairs={{0,4},{4,8},{8,12},{12,0},{1,5},{5,9},{9,13},{13,1},{2,6},{6,10},{... | collective-permute-start | bytes 3145736 | tf_op jit(solution)/shard_map/ppermute | solution.py:39
  9.6 151.4 %reduce-scatter.2.cloned.1.call-start = ((), (), s32[]{:S(2)}) async-start(), calls=%async_computation.2 | async-start | bytes 5242880 | tf_op jit(solution)/shard_map/reduce_scatter | solution.py:44
  35.1 26.1 %collective-permute-start.1 = (f32[1024,256]{1,0:T(8,128)S(1)}, f32[1024,256]{1,0:T(8,128)S(1)}, u32[]{:S(2)}, u32[]{:S(2)}) collective-permute-start(f32[1024,256]{1,0:T(8,128)S(1)} %collective-permute-done), channel_id=1, source_target_pairs={{0,4},{4,8},{8,12},{12,0},{1,5},{5,9},{9,13},{13,1},{2,6},{6,10},{... | collective-permute-start | bytes 3145736 | tf_op jit(solution)/shard_map/ppermute | solution.py:39
  61.2 25.4 %collective-permute-start.2 = (f32[1024,256]{1,0:T(8,128)S(1)}, f32[1024,256]{1,0:T(8,128)}, u32[]{:S(2)}, u32[]{:S(2)}) collective-permute-start(f32[1024,256]{1,0:T(8,128)S(1)} %collective-permute-done.1), channel_id=1, source_target_pairs={{0,4},{4,8},{8,12},{12,0},{1,5},{5,9},{9,13},{13,1},{2,6},{6,10},{... | collective-permute-start | bytes 3145736 | tf_op jit(solution)/shard_map/ppermute | solution.py:39
  98.0 2.4 %copy-start.1 = (f32[1024,1024]{1,0:T(8,128)S(1)}, f32[1024,1024]{1,0:T(8,128)}, u32[]{:S(2)}) copy-start(f32[1024,1024]{1,0:T(8,128)} %all-gather.2.cloned.1.call-done) | copy-start | bytes 12582916
Sparse Core Ops, SparseCore 0:
  9.7 58.5 all-gather.1
  118.5 42.4 reduce-scatter.1
